TPU v7x, 128 devices: a whole 4x4x4 slice. The times are simulated.
128 devices in a mesh: space: 16 (over z_lo, y, core), mode: 8 (over x, z_hi).
Axes of the slice: x: 4, y: 4, z: 4 (z_hi: 2, z_lo: 2; z = z_hi * 2 + z_lo), core: 2. Of those that a mesh axis runs over, the one named last changes fastest.
Arguments:
- test_modes: float32 [32, 3, 8, 32, 256], P(None, None, None, 'space'), may hold values from -6 to 6
- modes: float32 [128, 3, 8, 32, 256], P('mode', None, None, 'space'), may hold values from -6 to 6
Outputs:
- triad: float32 [32, 128, 128], P('space', 'mode')
All inputs are finite; a program needn't handle non-finite values.
Results may differ from a plain program's by a relative error of at most 0.000071.
Values sent between devices are 32-bit elements; how exact they have to be, the bound alone decides.
A program may use at most 64 MiB of HBM per device.

v0:
```python
import math
import jax
import jax.numpy as jnp
from jax import lax
from jax.sharding import PartitionSpec as P

MODES = 128
NX = 256
NZ = 8
BLOCK = 2048


def extended(value, sides, width):
    for axis, dim in sides:
        size, length = (lax.axis_size(axis), value.shape[dim])
        up = [(i, (i + 1) % size) for i in range(size)]
        down = [(j, i) for i, j in up]
        last = lax.slice_in_dim(value, length - width, length, axis=dim)
        leading = lax.slice_in_dim(value, 0, width, axis=dim)
        before = lax.ppermute(last, axis, up)
        after = lax.ppermute(leading, axis, down)
        value = jnp.concatenate([before, value, after], axis=dim)
    return value


def in_blocks(value, dim, size):
    shape = value.shape
    parts = value.reshape(*shape[:dim], size, shape[dim] // size, *shape[dim + 1 :])
    return jnp.moveaxis(parts, dim, 0)


def sent_and_summed(value, axis, dim):
    parts = in_blocks(value, dim, lax.axis_size(axis))
    arrived = lax.all_to_all(parts, axis, split_axis=0, concat_axis=0, tiled=True)
    return arrived.sum(axis=0)


def central_diff(field, along):
    ahead = jnp.roll(field, -1, along) - jnp.roll(field, 1, along)
    farther = jnp.roll(field, -2, along) - jnp.roll(field, 2, along)
    return (8.0 * ahead - farther) / 12.0


def per_device(test_modes, modes):
    local_count = modes.shape[0]
    test_count = test_modes.shape[0]
    row_count = modes.shape[3]
    padded = extended(modes, (("space", 3),), 2)
    ahead = padded[:, :, :, 3 : row_count + 3] - padded[:, :, :, 1 : row_count + 1]
    farther = padded[:, :, :, 4 : row_count + 4] - padded[:, :, :, 0:row_count]
    along_y = (8.0 * ahead - farther) / 12.0
    gradients = jnp.stack([central_diff(modes, 4), along_y, central_diff(modes, 2)], axis=2)
    gradients = gradients.reshape(local_count, 3, 3, -1)
    test_flat = test_modes.reshape(test_count, 3, -1)
    mode_flat = modes.reshape(local_count, 3, -1)
    cell_count = test_flat.shape[2]
    block_count = cell_count // BLOCK
    volume_scale = 1.0 / math.sqrt(NX * NZ * row_count * lax.axis_size("space"))

    def weigh(offset):
        test_block = lax.dynamic_slice_in_dim(test_flat, offset, BLOCK, 2)
        grad_block = lax.dynamic_slice_in_dim(gradients, offset, BLOCK, 3)
        weighted = test_block[:, 0, None, None, :] * grad_block[None, :, 0]
        weighted = weighted + test_block[:, 1, None, None, :] * grad_block[None, :, 1]
        weighted = weighted + test_block[:, 2, None, None, :] * grad_block[None, :, 2]
        return weighted

    def add_piece(running, weighted, piece_block):
        partial_value = jnp.einsum(
            "ikbc,jbc->ikj", weighted, piece_block, precision=lax.Precision.HIGHEST
        )
        return running + partial_value

    initial = jnp.zeros((test_count, local_count, MODES), jnp.float32)
    everything = lax.all_gather(mode_flat, "mode", axis=0, tiled=True)

    def one_block(index_block, running):
        offset = index_block * BLOCK
        weighted = weigh(offset)
        piece_block = lax.dynamic_slice_in_dim(everything, offset, BLOCK, 2)
        return add_piece(running, weighted, piece_block)

    partial_triad = lax.fori_loop(0, block_count, one_block, initial)
    partial_triad = partial_triad * volume_scale
    result = sent_and_summed(partial_triad, "space", 0)
    return result


def solution(mesh):
    in_specs = (P(None, None, None, "space", None), P("mode", None, None, "space", None))
    out_specs = P("space", "mode", None)
    return jax.shard_map(
        per_device, mesh=mesh, in_specs=in_specs, out_specs=out_specs, check_vma=False
    )
```

profile of v0, /device:TPU:1, one launch (start us, length us, event | category | flops | bytes accessed | tf_op | source)
XLA Modules:
  0.0 155.8 jit_solution(17726550223214487848)
XLA Ops:
  6.5 0.0 copy-start
  6.5 0.0 all-gather.2.cloned.1.call-start
  6.5 1.5 copy.22
  8.1 1.6 %reshape.137 = f32[16,3,4096]{2,0,1:T(8,128)} reshape(f32[16,3,8,2,256]{4,3,2,0,1:T(2,128)S(1)} %copy.22) | data formatting | bytes 1572864 | tf_op jit(solution)/shard_map/reshape | solution.py:55
  9.7 0.0 all-gather.2.cloned.1.call-update
  9.7 1.5 collective-permute-start
  11.1 1.4 collective-permute-start.1
  12.5 1.6 %fusion.35 = (f32[16,3,8,2,1]{4,3,2,1,0:T(2,128)S(1)}, f32[16,3,8,2,1]{4,3,2,1,0:T(2,128)S(1)}) fusion(f32[16,3,8,2,256]{4,3,2,1,0:T(2,128)} %param.5), kind=kLoop, calls=%fused_computation.55 | loop fusion | bytes 12288 | tf_op jit(solution)/shard_map/jit(_roll_static)/slice | solution.py:39
  14.1 0.4 copy.24
  14.5 0.4 copy.14
  14.9 0.4 copy.25
  15.3 0.4 copy.16
  15.7 0.0 copy-done
  15.7 0.5 slice_bitcast_fusion.8
  16.3 1.1 slice_bitcast_fusion
  17.3 1.1 slice_bitcast_fusion.2
  18.4 3.2 %fusion.30 = f32[16,3,1,8,2,256]{5,4,3,1,0,2:T(2,128)S(1)} fusion(f32[16,3,1,8,2,1]{5,4,3,1,0,2:T(2,128)S(1)} %copy.14, f32[16,3,1,8,2,255]{5,4,3,1,0,2:T(2,128)S(1)} %get-tuple-element.141, f32[16,3,1,8,2,255]{5,4,3,1,0,2:T(2,128)S(1)} %get-tuple-element.140, f32[16,3,1,8,2,1]{5,4,3,1,0,2:T(2,128)S(1)} %copy.16, ...), kind=kLoop, calls=%fused_computation.32 | loop fusion | flops 1769472 | bytes 3932160 | tf_op jit(solution)/shard_map/div | solution.py:41
  21.7 0.3 copy.17
  21.9 0.6 div.14
  22.6 0.1 slice_bitcast_fusion.10
  22.7 0.3 slice_bitcast_fusion.6
  23.1 0.4 slice_bitcast_fusion.4
  23.5 1.3 fusion.33
  24.8 0.3 copy.21
  25.2 1.6 %div.17 = f32[16,3,1,4096]{3,0,2,1:T(8,128)} reshape(f32[16,3,1,8,2,256]{5,4,3,0,1,2:T(2,128)S(1)} %copy.21) | data formatting | bytes 1572864 | tf_op jit(solution)/shard_map/div | solution.py:41
  26.8 2.1 %copy.12 = f32[32,3,8,2,256]{4,3,2,0,1:T(2,128)S(1)} copy(f32[32,3,8,2,256]{4,3,2,1,0:T(2,128)} %param.4) | data formatting | bytes 3145728 | tf_op args[0]
  28.9 2.4 %reshape.136 = f32[32,3,4096]{2,0,1:T(8,128)} reshape(f32[32,3,8,2,256]{4,3,2,0,1:T(2,128)S(1)} %copy.12) | data formatting | bytes 3145728 | tf_op jit(solution)/shard_map/reshape | solution.py:54
  31.3 0.0 collective-permute-done
  31.3 0.0 collective-permute-done.1
  31.3 3.9 %fusion.34 = f32[16,3,8,2,256]{4,3,2,1,0:T(2,128)S(1)} fusion(f32[16,3,8,2,256]{4,3,2,1,0:T(2,128)} %collective-permute-done, f32[16,3,8,2,256]{4,3,2,1,0:T(2,128)} %collective-permute-done.1, f32[16,3,8,2,256]{4,3,2,1,0:T(2,128)S(1)} %copy-done), kind=kLoop, calls=%fused_computation.43 | loop fusion | flops 1376256 | bytes 3145728 | tf_op jit(solution)/shard_map/div | solution.py:51
  35.2 0.3 copy.18
  35.6 1.5 stack.8
  37.1 1.5 pad_maximum_fusion
  38.7 62.8 %all-gather.2.cloned.1.call-done = f32[128,3,4096]{2,0,1:T(8,128)} async-done(((f32[16,3,4096]{2,0,1:T(8,128)}), f32[128,3,4096]{2,0,1:T(8,128)}) %all-gather.2.cloned.1.call-update) | async-done | bytes 6291472 | tf_op jit(solution)/shard_map/all_gather | solution.py:75
  101.5 33.1 %while.14 = (s32[]{:T(128)}, f32[32,16,128]{2,1,0:T(8,128)}, f32[32,3,4096]{2,0,1:T(8,128)}, f32[16,3,3,4096]{3,0,2,1:T(8,128)S(1)}, f32[128,3,4096]{2,0,1:T(8,1...) while((s32[]{:T(128)}, f32[32,16,128]{2,1,0:T(8,128)}, ...), condition=%wide.region_1.2_spmd.clone, body=%wide.region_0.1_spmd.clone.sunk | while | flops 4847697920 | bytes 9568473 | solution.py:83
  101.5 0.1 dynamic-slice_bitcast_fusion.8
  101.6 2.1 %dynamic-slice_bitcast_fusion.9 = (f32[32,2048]{1,0:T(8,128)}, f32[32,2048]{1,0:T(8,128)}, f32[32,2048]{1,0:T(8,128)}) fusion(f32[32,3,4096]{2,0,1:T(8,128)} %get-tuple-element.217, s32[]{:T(128)S(6)} %select_n.11, s32[]{:T(128)S(6)} %add.82, s32[]{:T(128)S(6)} %add.83), kind=kLoop, calls=%fused_computation.21.clone.1 | loop fusion | bytes 1572876 | tf_op jit(solution)/shard_map/while/body/eval_jaxpr/mul | solution.py:63
  103.7 14.3 %fusion.41 = f32[32,16,128]{2,1,0:T(8,128)} fusion(f32[128,3,4096]{2,0,1:T(8,128)} %get-tuple-element.219, s32[]{:T(128)S(6)} %select_n.11, f32[16,3,2048]{2,0,1:T(8,128)S(1)} %get-tuple-element.187, f32[32,2048]{1,0:T(8,128)} %get-tuple-element.188, f32[16,3,2048]{2,0,1:T(8,128)S(1)} %get-tuple-element.189, f32[32,2048]{1,0:T(8,128)} %get-tuple-element.190, ...), kind=kOutput, calls=%fused_computation.15.clone.1 | convolution fusion | flops 4847697920 | bytes 5636101 | tf_op jit(solution)/shard_map/while/body/eval_jaxpr/ikbc,jbc->ikj/dot_general | solution.py:69
  118.0 0.1 dynamic-slice_bitcast_fusion.8
  118.1 2.1 %dynamic-slice_bitcast_fusion.9 = (f32[32,2048]{1,0:T(8,128)}, f32[32,2048]{1,0:T(8,128)}, f32[32,2048]{1,0:T(8,128)}) fusion(f32[32,3,4096]{2,0,1:T(8,128)} %get-tuple-element.217, s32[]{:T(128)S(6)} %select_n.11, s32[]{:T(128)S(6)} %add.82, s32[]{:T(128)S(6)} %add.83), kind=kLoop, calls=%fused_computation.21.clone.1 | loop fusion | bytes 1572876 | tf_op jit(solution)/shard_map/while/body/eval_jaxpr/mul | solution.py:63
  120.2 14.3 %fusion.41 = f32[32,16,128]{2,1,0:T(8,128)} fusion(f32[128,3,4096]{2,0,1:T(8,128)} %get-tuple-element.219, s32[]{:T(128)S(6)} %select_n.11, f32[16,3,2048]{2,0,1:T(8,128)S(1)} %get-tuple-element.187, f32[32,2048]{1,0:T(8,128)} %get-tuple-element.188, f32[16,3,2048]{2,0,1:T(8,128)S(1)} %get-tuple-element.189, f32[32,2048]{1,0:T(8,128)} %get-tuple-element.190, ...), kind=kOutput, calls=%fused_computation.15.clone.1 | convolution fusion | flops 4847697920 | bytes 5636101 | tf_op jit(solution)/shard_map/while/body/eval_jaxpr/ikbc,jbc->ikj/dot_general | solution.py:69
  134.6 1.0 broadcast_multiply_fusion
  135.5 12.8 %all_to_all.5 = f32[16,2,16,128]{3,2,1,0:T(8,128)S(1)} all-to-all(f32[16,2,16,128]{3,2,1,0:T(8,128)S(1)} %bitcast.77), channel_id=1, replica_groups=mesh['space'=16,'mode'=8] {'space'}, dimensions={0} | all-to-all | bytes 524288 | tf_op jit(solution)/shard_map/all_to_all | solution.py:34
  148.3 0.6 reduce_sum.9
  (2 shorter events, 0.0 us)
Async XLA Ops:
  6.5 9.2 %copy-start = (f32[16,3,8,2,256]{4,3,2,1,0:T(2,128)S(1)}, f32[16,3,8,2,256]{4,3,2,1,0:T(2,128)}, u32[]{:S(2)}) copy-start(f32[16,3,8,2,256]{4,3,2,1,0:T(2,128)} %param.5) | copy-start | bytes 2359300
  6.5 94.9 %all-gather.2.cloned.1.call-start = ((), (), s32[]{:S(2)}) async-start(), calls=%async_computation.1 | async-start | bytes 7077888 | tf_op jit(solution)/shard_map/all_gather | solution.py:75
  9.7 21.6 %collective-permute-start = (f32[16,3,8,2,256]{4,3,2,1,0:T(2,128)}, f32[16,3,8,2,256]{4,3,2,1,0:T(2,128)}, u32[]{:S(2)}, u32[]{:S(2)}) collective-permute-start(f32[16,3,8,2,256]{4,3,2,1,0:T(2,128)} %param.5), channel_id=1, source_target_pairs={{8,0},{16,8},{24,16},{32,24},{40,32},{48,40},{56,48},{64,56},{72,6... | collective-permute-start | bytes 2359304 | tf_op jit(solution)/shard_map/ppermute | solution.py:21
  11.1 20.2 %collective-permute-start.1 = (f32[16,3,8,2,256]{4,3,2,1,0:T(2,128)}, f32[16,3,8,2,256]{4,3,2,1,0:T(2,128)}, u32[]{:S(2)}, u32[]{:S(2)}) collective-permute-start(f32[16,3,8,2,256]{4,3,2,1,0:T(2,128)} %param.5), channel_id=1, source_target_pairs={{0,8},{8,16},{16,24},{24,32},{32,40},{40,48},{48,56},{56,64},{64,7... | collective-permute-start | bytes 2359304 | tf_op jit(solution)/shard_map/ppermute | solution.py:20
Sparse Core Ops, SparseCore 0:
  9.8 91.6 all-gather.1
where the time goes:
time: 156 us
  waiting for transfers between devices  62.9 us (40%)
  matrix products  28.6 us (18%)
  local copies, waits for them, and re-layouts  23.5 us (15%)
  between operations  13.5 us (9%)
  blocking collectives  12.8 us (8%)
  other arithmetic  11.7 us (8%)
  starting transfers between devices  2.83 us (2%)
    all_gather x1, waiting for transfers between devices, per_device(): everything = lax.all_gather(mode_flat, 'mode', axis=0, tiled=True)  62.8 us
    dot_general x2, matrix products, add_piece(): jnp.einsum('ikbc,jbc->ikj', weighted, piece_block, precision=lax.Precisio...  28.6 us
    all_to_all x1, blocking collectives, sent_and_summed(): lax.all_to_all(parts, axis, split_axis=0, concat_axis=0, tiled=True)  12.8 us
    div x2, other arithmetic, central_diff(): return (8.0 * ahead - farther) / 12.0  4.57 us
    mul x4, local copies, waits for them, and re-layouts, weigh(): weighted = test_block[:, 0, None, None, :] * grad_block[None, :, 0]  4.42 us
    unnamed x6, local copies, waits for them, and re-layouts  4.36 us
    div x1, other arithmetic, per_device(): along_y = (8.0 * ahead - farther) / 12.0  3.94 us
  transfers between devices with their start and end apart: 3, of which 1 were waited for; matrix products, arithmetic and copies ran while one was open for 17% of the time, Pallas kernels for 0%

commit v1 on v0

--- a/solution.py
+++ b/solution.py
@@ -72,7 +72,10 @@
         return running + partial_value
 
     initial = jnp.zeros((test_count, local_count, MODES), jnp.float32)
-    everything = lax.all_gather(mode_flat, "mode", axis=0, tiled=True)
+    count = lax.axis_size("mode")
+    blocks = jnp.stack([mode_flat for _ in range(count)])
+    blocks = lax.all_to_all(blocks, "mode", split_axis=0, concat_axis=0)
+    everything = jnp.concatenate(blocks, axis=0)
 
     def one_block(index_block, running):
         offset = index_block * BLOCK

time: 156 us -> 164 us (1.051)
  between operations: 13.5 us -> 0.17 us
  starting transfers between devices: 2.83 us -> 10.6 us
  local copies, waits for them, and re-layouts: 23.5 us -> 30.7 us
  waiting for transfers between devices: 62.9 us -> 68.3 us
    all_to_all x0 -> x1, waiting for transfers between devices: none -> 68.3 us  [per_device(): blocks = lax.all_to_all(blocks, 'mode', split_axis=0, concat_axis=0)]
    all_gather x1 -> x0, waiting for transfers between devices: 62.8 us -> none  [per_device(): everything = lax.all_gather(mode_flat, 'mode', axis=0, tiled=True)]
    all_to_all x0 -> x1, starting transfers between devices: none -> 8.28 us  [per_device(): blocks = lax.all_to_all(blocks, 'mode', split_axis=0, concat_axis=0)]
    all_to_all x0 -> x1, local copies, waits for them, and re-layouts: none -> 6.14 us  [per_device(): blocks = lax.all_to_all(blocks, 'mode', split_axis=0, concat_axis=0)]
    another operation x0 -> x2, local copies, waits for them, and re-layouts: none -> 4.02 us  [per_device(): blocks = jnp.stack([mode_flat for _ in range(count)])]
  transfers between devices with their start and end apart: 3 -> 3, of which waited for: 1 -> 1; matrix products, arithmetic and copies ran while one was open for 17% -> 15% of each run, Pallas kernels for 0% -> 0%
where the time goes in v1:
time: 164 us; the launch traced here: 163 us
  waiting for transfers between devices  68.3 us (42%)
  local copies, waits for them, and re-layouts  30.7 us (19%)
  matrix products  28.6 us (17%)
  blocking collectives  13.3 us (8%)
  other arithmetic  11.6 us (7%)
  starting transfers between devices  10.6 us (6%)
    all_to_all x1, waiting for transfers between devices, per_device(): blocks = lax.all_to_all(blocks, 'mode', split_axis=0, concat_axis=0)  68.3 us
    dot_general x2, matrix products, add_piece(): jnp.einsum('ikbc,jbc->ikj', weighted, piece_block, precision=lax.Precisio...  28.6 us
    all_to_all x1, blocking collectives, sent_and_summed(): lax.all_to_all(parts, axis, split_axis=0, concat_axis=0, tiled=True)  13.3 us
    all_to_all x1, starting transfers between devices, per_device(): blocks = lax.all_to_all(blocks, 'mode', split_axis=0, concat_axis=0)  8.28 us
    all_to_all x1, local copies, waits for them, and re-layouts, per_device(): blocks = lax.all_to_all(blocks, 'mode', split_axis=0, concat_axis=0)  6.14 us
    div x2, other arithmetic, central_diff(): return (8.0 * ahead - farther) / 12.0  4.57 us
    mul x4, local copies, waits for them, and re-layouts, weigh(): weighted = test_block[:, 0, None, None, :] * grad_block[None, :, 0]  4.32 us
    unnamed x6, local copies, waits for them, and re-layouts  4.29 us
  transfers between devices with their start and end apart: 3, of which 1 were waited for; matrix products, arithmetic and copies ran while one was open for 15% of the time, Pallas kernels for 0%

profile of v1, /device:TPU:1, one launch (start us, length us, event | category | flops | bytes accessed | tf_op | source)
XLA Modules:
  0.0 163.3 jit_solution(15833085106199229647)
XLA Ops:
  0.0 1.4 copy.44
  1.5 0.6 stack_reshape.2
  2.1 3.4 %stack.13 = f32[8,16,3,4096]{3,1,2,0:T(8,128)} broadcast(f32[16,3,4096]{2,0,1:T(8,128)S(1)} %stack_reshape.2), dimensions={1,2,3} | broadcast | bytes 7077888 | tf_op jit(solution)/shard_map/stack | solution.py:76
  5.5 0.0 copy-start
  5.5 8.3 %all-to-all-start = ((f32[8,16,3,4096]{3,1,2,0:T(8,128)}), f32[8,16,3,4096]{3,1,2,0:T(8,128)}, u32[]{:S(2)}, u32[]{:S(2)}) async-start(f32[8,16,3,4096]{3,1,2,0:T(8,128)} %stack.13), calls=%async_computation | async-start | bytes 12582912 | tf_op jit(solution)/shard_map/all_to_all | solution.py:77
  13.8 0.0 copy-done
  13.8 1.0 collective-permute-start
  14.8 1.3 collective-permute-start.1
  16.1 0.5 fusion.35
  16.6 0.4 copy.47
  17.0 0.4 copy.36
  17.4 0.4 copy.48
  17.8 0.4 copy.38
  18.2 0.5 slice_bitcast_fusion.8
  18.7 1.1 slice_bitcast_fusion
  19.8 1.1 slice_bitcast_fusion.2
  20.9 3.2 %fusion.30 = f32[16,3,1,8,2,256]{5,4,3,1,0,2:T(2,128)S(1)} fusion(f32[16,3,1,8,2,1]{5,4,3,1,0,2:T(2,128)S(1)} %copy.36, f32[16,3,1,8,2,255]{5,4,3,1,0,2:T(2,128)S(1)} %get-tuple-element.141, f32[16,3,1,8,2,255]{5,4,3,1,0,2:T(2,128)S(1)} %get-tuple-element.140, f32[16,3,1,8,2,1]{5,4,3,1,0,2:T(2,128)S(1)} %copy.38, ...), kind=kLoop, calls=%fused_computation.32 | loop fusion | flops 1769472 | bytes 3932160 | tf_op jit(solution)/shard_map/div | solution.py:41
  24.1 0.3 copy.39
  24.4 0.6 div.14
  25.1 0.1 slice_bitcast_fusion.10
  25.2 0.3 slice_bitcast_fusion.6
  25.6 0.4 slice_bitcast_fusion.4
  26.0 1.3 fusion.33
  27.3 0.3 copy.43
  27.6 1.5 div.17
  29.2 2.1 %copy.34 = f32[32,3,8,2,256]{4,3,2,0,1:T(2,128)S(1)} copy(f32[32,3,8,2,256]{4,3,2,1,0:T(2,128)} %param.4) | data formatting | bytes 3145728 | tf_op args[0]
  31.3 2.4 %reshape.138 = f32[32,3,4096]{2,0,1:T(8,128)} reshape(f32[32,3,8,2,256]{4,3,2,0,1:T(2,128)S(1)} %copy.34) | data formatting | bytes 3145728 | tf_op jit(solution)/shard_map/reshape | solution.py:54
  33.7 0.0 collective-permute-done
  33.7 0.0 collective-permute-done.1
  33.7 3.9 %fusion.34 = f32[16,3,8,2,256]{4,3,2,1,0:T(2,128)S(1)} fusion(f32[16,3,8,2,256]{4,3,2,1,0:T(2,128)} %collective-permute-done, f32[16,3,8,2,256]{4,3,2,1,0:T(2,128)} %collective-permute-done.1, f32[16,3,8,2,256]{4,3,2,1,0:T(2,128)S(1)} %copy-done), kind=kLoop, calls=%fused_computation.43 | loop fusion | flops 1376256 | bytes 3145728 | tf_op jit(solution)/shard_map/div | solution.py:51
  37.6 0.3 copy.40
  37.9 1.5 stack.11
  39.4 1.5 pad_maximum_fusion
  41.0 68.3 %all-to-all-done = f32[8,16,3,4096]{3,1,2,0:T(8,128)} async-done(((f32[8,16,3,4096]{3,1,2,0:T(8,128)}), f32[8,16,3,4096]{3,1,2,0:T(8,128)}, u32[]{:S(2)}, u32[]{:S(2)}) %all-to-all-start) | async-done | bytes 6291488 | tf_op jit(solution)/shard_map/all_to_all | solution.py:77
  109.3 6.1 %copy.45 = f32[8,16,3,4096]{3,1,0,2:T(8,128)} copy(f32[8,16,3,4096]{3,1,2,0:T(8,128)} %all-to-all-done) | data formatting | bytes 12582912 | tf_op jit(solution)/shard_map/all_to_all | solution.py:77
  115.4 32.9 %while.14 = (s32[]{:T(128)}, f32[32,16,128]{2,1,0:T(8,128)}, f32[32,3,4096]{2,0,1:T(8,128)}, f32[16,3,3,4096]{3,0,2,1:T(8,128)S(1)}, f32[128,3,4096]{2,0,1:T(8,1...) while((s32[]{:T(128)}, f32[32,16,128]{2,1,0:T(8,128)}, ...), condition=%wide.region_1.2_spmd.clone, body=%wide.region_0.1_spmd.clone.sunk | while | flops 4847697920 | bytes 9568473 | solution.py:86
  115.4 0.1 dynamic-slice_bitcast_fusion.8
  115.5 2.1 %dynamic-slice_bitcast_fusion.9 = (f32[32,2048]{1,0:T(8,128)}, f32[32,2048]{1,0:T(8,128)}, f32[32,2048]{1,0:T(8,128)}) fusion(f32[32,3,4096]{2,0,1:T(8,128)} %get-tuple-element.217, s32[]{:T(128)S(6)} %select_n.11, s32[]{:T(128)S(6)} %add.82, s32[]{:T(128)S(6)} %add.83), kind=kLoop, calls=%fused_computation.21.clone.1 | loop fusion | bytes 1572876 | tf_op jit(solution)/shard_map/while/body/eval_jaxpr/mul | solution.py:63
  117.6 14.3 %fusion.41 = f32[32,16,128]{2,1,0:T(8,128)} fusion(f32[128,3,4096]{2,0,1:T(8,128)} %get-tuple-element.219, s32[]{:T(128)S(6)} %select_n.11, f32[16,3,2048]{2,0,1:T(8,128)S(1)} %get-tuple-element.187, f32[32,2048]{1,0:T(8,128)} %get-tuple-element.188, f32[16,3,2048]{2,0,1:T(8,128)S(1)} %get-tuple-element.189, f32[32,2048]{1,0:T(8,128)} %get-tuple-element.190, ...), kind=kOutput, calls=%fused_computation.15.clone.1 | convolution fusion | flops 4847697920 | bytes 5636101 | tf_op jit(solution)/shard_map/while/body/eval_jaxpr/ikbc,jbc->ikj/dot_general | solution.py:69
  131.9 0.1 dynamic-slice_bitcast_fusion.8
  132.0 2.1 %dynamic-slice_bitcast_fusion.9 = (f32[32,2048]{1,0:T(8,128)}, f32[32,2048]{1,0:T(8,128)}, f32[32,2048]{1,0:T(8,128)}) fusion(f32[32,3,4096]{2,0,1:T(8,128)} %get-tuple-element.217, s32[]{:T(128)S(6)} %select_n.11, s32[]{:T(128)S(6)} %add.82, s32[]{:T(128)S(6)} %add.83), kind=kLoop, calls=%fused_computation.21.clone.1 | loop fusion | bytes 1572876 | tf_op jit(solution)/shard_map/while/body/eval_jaxpr/mul | solution.py:63
  134.1 14.3 %fusion.41 = f32[32,16,128]{2,1,0:T(8,128)} fusion(f32[128,3,4096]{2,0,1:T(8,128)} %get-tuple-element.219, s32[]{:T(128)S(6)} %select_n.11, f32[16,3,2048]{2,0,1:T(8,128)S(1)} %get-tuple-element.187, f32[32,2048]{1,0:T(8,128)} %get-tuple-element.188, f32[16,3,2048]{2,0,1:T(8,128)S(1)} %get-tuple-element.189, f32[32,2048]{1,0:T(8,128)} %get-tuple-element.190, ...), kind=kOutput, calls=%fused_computation.15.clone.1 | convolution fusion | flops 4847697920 | bytes 5636101 | tf_op jit(solution)/shard_map/while/body/eval_jaxpr/ikbc,jbc->ikj/dot_general | solution.py:69
  148.3 1.0 broadcast_multiply_fusion
  149.3 13.3 %all_to_all.10 = f32[16,2,16,128]{3,2,1,0:T(8,128)S(1)} all-to-all(f32[16,2,16,128]{3,2,1,0:T(8,128)S(1)} %bitcast.79), channel_id=1, replica_groups=mesh['space'=16,'mode'=8] {'space'}, dimensions={0} | all-to-all | bytes 524288 | tf_op jit(solution)/shard_map/all_to_all | solution.py:34
  162.6 0.6 reduce_sum.9
  (2 shorter events, 0.0 us)
Async XLA Ops:
  5.5 8.3 %copy-start = (f32[16,3,8,2,256]{4,3,2,1,0:T(2,128)S(1)}, f32[16,3,8,2,256]{4,3,2,1,0:T(2,128)}, u32[]{:S(2)}) copy-start(f32[16,3,8,2,256]{4,3,2,1,0:T(2,128)} %param.5) | copy-start | bytes 2359300
  5.5 103.8 %all-to-all-start = ((f32[8,16,3,4096]{3,1,2,0:T(8,128)}), f32[8,16,3,4096]{3,1,2,0:T(8,128)}, u32[]{:S(2)}, u32[]{:S(2)}) async-start(f32[8,16,3,4096]{3,1,2,0:T(8,128)} %stack.13), calls=%async_computation | async-start | bytes 12582912 | tf_op jit(solution)/shard_map/all_to_all | solution.py:77
  13.8 19.9 %collective-permute-start = (f32[16,3,8,2,256]{4,3,2,1,0:T(2,128)S(1)}, f32[16,3,8,2,256]{4,3,2,1,0:T(2,128)}, u32[]{:S(2)}, u32[]{:S(2)}) collective-permute-start(f32[16,3,8,2,256]{4,3,2,1,0:T(2,128)S(1)} %copy-done), channel_id=1, source_target_pairs={{8,0},{16,8},{24,16},{32,24},{40,32},{48,40},{56,48},{64,56},{72,6... | collective-permute-start | bytes 2359304 | tf_op jit(solution)/shard_map/ppermute | solution.py:21
  14.8 18.9 %collective-permute-start.1 = (f32[16,3,8,2,256]{4,3,2,1,0:T(2,128)S(1)}, f32[16,3,8,2,256]{4,3,2,1,0:T(2,128)}, u32[]{:S(2)}, u32[]{:S(2)}) collective-permute-start(f32[16,3,8,2,256]{4,3,2,1,0:T(2,128)S(1)} %copy-done), channel_id=1, source_target_pairs={{0,8},{8,16},{16,24},{24,32},{32,40},{40,48},{48,56},{56,64},{64,7... | collective-permute-start | bytes 2359304 | tf_op jit(solution)/shard_map/ppermute | solution.py:20
